TPU v7x, 32 devices: a whole 2x2x4 slice. The times are simulated.
32 devices in a mesh: tok: 16 (over z, y, x), blk: 2 (over core).
Axes of the slice: x: 2, y: 2, z: 4, core: 2. Of those that a mesh axis runs over, the one named last changes fastest.
Arguments:
- activations: bfloat16 [4096, 2048], P('tok', 'blk'), may hold values from -16 to 16
Outputs:
- factored: float32 [2048, 2048], P('blk', 'tok')
All inputs are finite; a program needn't handle non-finite values.
Results may differ from a plain program's by a relative error of at most 0.0003.
Values may be sent and summed in bfloat16 or wider, within the bound.
A program may use at most 64 MiB of HBM per device.

v0:
```python
import jax
import jax.numpy as jnp
from jax import lax
from jax.sharding import PartitionSpec as P

STEPS = 4


def spread(block, axis, holder):
    block = jnp.where(lax.axis_index(axis) == holder, block, jnp.zeros_like(block))
    return lax.psum(block, axis)


def shards(activations):
    rows_block = activations.shape[1]
    tok_count = lax.axis_size("tok")
    blk_count = lax.axis_size("blk")
    full_width = rows_block * blk_count
    strip_width = full_width // tok_count
    total_tokens = activations.shape[0] * tok_count
    partial_rows = lax.dot_general(
        activations,
        lax.all_gather(activations, "blk", axis=1, tiled=True),
        (((0,), (0,)), ((), ())),
        preferred_element_type=jnp.float32,
    )
    pieces = lax.all_to_all(partial_rows, "tok", split_axis=1, concat_axis=0, tiled=True)
    hessian_tile = jnp.sum(pieces.reshape(tok_count, rows_block, strip_width), axis=0) * (
        2.0 / total_tokens
    )
    tok_index = lax.axis_index("tok")
    blk_index = lax.axis_index("blk")
    row_ids = blk_index * rows_block + jnp.arange(rows_block, dtype=jnp.int32)[:, None]
    col_ids = tok_index * strip_width + jnp.arange(strip_width, dtype=jnp.int32)[None, :]
    on_diag = row_ids == col_ids
    trace_total = lax.psum(jnp.sum(jnp.where(on_diag, hessian_tile, 0.0)), ("tok", "blk"))
    hessian_tile = hessian_tile + jnp.where(on_diag, 0.01 * trace_total / full_width, 0.0)
    positions = jnp.arange(full_width, dtype=jnp.int32)[:, None]
    for section in range(STEPS):
        strip_rows = spread(hessian_tile, "tok", section)
        column = lax.all_gather(strip_rows, "blk", axis=0, tiled=True)
        pivot_block = column[section * strip_width : (section + 1) * strip_width]
        factor = jnp.linalg.cholesky(pivot_block)
        solved = jax.scipy.linalg.solve_triangular(factor, column.T, lower=True).T
        solved = jnp.where(positions >= section * strip_width, solved, 0.0)
        own_rows = lax.dynamic_slice_in_dim(solved, blk_index * rows_block, rows_block, 0)
        own_cols = lax.dynamic_slice_in_dim(solved, tok_index * strip_width, strip_width, 0)
        update = jnp.dot(own_rows, own_cols.T, precision=lax.Precision.HIGHEST)
        hessian_tile = jnp.where(
            tok_index > section,
            hessian_tile - update,
            jnp.where(tok_index == section, own_rows, hessian_tile),
        )
    return jnp.where(row_ids >= col_ids, hessian_tile, 0.0)


def solution(mesh):
    return jax.shard_map(
        shards, mesh=mesh, in_specs=(P("tok", "blk"),), out_specs=P("blk", "tok"), check_vma=False
    )
```

profile of v0, /device:TPU:0, one launch (start us, length us, event | category | flops | bytes accessed | tf_op | source)
XLA Modules:
  0.0 871.7 jit_solution(5197727431388348437)
XLA Ops:
  7.3 13.4 %all-gather.6.cloned.1.call-done = bf16[256,2048]{1,0:T(8,128)(2,1)} async-done(((bf16[256,1024]{1,0:T(8,128)(2,1)}), bf16[256,2048]{1,0:T(8,128)(2,1)}) %all-gather.6.cloned.1.call-update) | async-done | bytes 1048592 | tf_op jit(solution)/shard_map/all_gather | solution.py:23
  20.7 2.7 convolution_bitcast_fusion
  23.3 4.1 copy.30
  27.4 6.8 all-to-all-start
  34.3 159.2 %all-to-all-done = f32[1024,16,128]{2,0,1:T(8,128)} async-done(((f32[1024,16,128]{2,0,1:T(8,128)}), f32[1024,16,128]{2,0,1:T(8,128)}, u32[]{:S(2)}, u32[]{:S(2)}) %all-to-all-start) | async-done | bytes 8388640 | tf_op jit(solution)/shard_map/all_to_all | solution.py:27
  193.5 3.8 reduce_sum.18
  198.4 70.9 %psum.35 = f32[]{:T(128)} all-reduce(f32[]{:T(128)} %fusion.10), channel_id=1, replica_groups=mesh['tok'=16,'blk'=2] {'tok','blk'}, use_global_device_ids=true, to_apply=%region_2.3 | all-reduce | flops 1 | bytes 8 | tf_op jit(solution)/shard_map/psum | solution.py:36
  269.9 0.9 fusion.16
  270.9 110.8 %all-reduce.5.cloned.1.call-done = f32[1024,128]{0,1:T(8,128)} async-done(((f32[1024,128]{0,1:T(8,128)}), f32[1024,128]{0,1:T(8,128)}) %all-reduce.5.cloned.1.call-update) | async-done | bytes 524304 | tf_op jit(solution)/shard_map/psum | solution.py:11
  381.8 9.5 %all-gather.8.cloned.1.call-done = f32[2048,128]{0,1:T(8,128)} async-done(((f32[1024,128]{0,1:T(8,128)}), f32[2048,128]{0,1:T(8,128)}) %all-gather.8.cloned.1.call-update) | async-done | bytes 1048592 | tf_op jit(solution)/shard_map/all_gather | solution.py:41
  393.1 11.7 %cholesky.74 = f32[128,128]{1,0:T(8,128)S(1)} custom-call(f32[128,128]{1,0:T(8,128)S(1)} %fusion.28), custom_call_target="Cholesky" | custom-call | tf_op jit(solution)/shard_map/jit(cholesky)/cholesky | solution.py:43
  406.1 9.8 %custom-call.8 = f32[1,128,128]{1,2,0:T(8,128)S(1)} custom-call(f32[1,128,128]{2,1,0:T(8,128)S(1)} %fusion.17), custom_call_target="InvertDiagBlocksLowerTriangular" | custom-call | tf_op jit(solution)/shard_map/jit(_solve_triangular)/triangular_solve | solution.py:44
  416.0 2.3 fusion.8
  418.2 1.5 broadcast_select_fusion.2
  419.8 110.4 %all-reduce.7.cloned.1.call-done = f32[1024,128]{0,1:T(8,128)} async-done(((f32[1024,128]{0,1:T(8,128)}), f32[1024,128]{0,1:T(8,128)}) %all-reduce.7.cloned.1.call-update) | async-done | bytes 524304 | tf_op jit(solution)/shard_map/psum | solution.py:11
  530.4 9.2 %all-gather.10.cloned.1.call-done = f32[2048,128]{0,1:T(8,128)} async-done(((f32[1024,128]{0,1:T(8,128)}), f32[2048,128]{0,1:T(8,128)}) %all-gather.10.cloned.1.call-update) | async-done | bytes 1048592 | tf_op jit(solution)/shard_map/all_gather | solution.py:41
  541.4 11.7 %cholesky.85 = f32[128,128]{1,0:T(8,128)S(1)} custom-call(f32[128,128]{1,0:T(8,128)S(1)} %fusion.26), custom_call_target="Cholesky" | custom-call | tf_op jit(solution)/shard_map/jit(cholesky)/cholesky | solution.py:43
  554.5 9.8 %custom-call.9 = f32[1,128,128]{1,2,0:T(8,128)S(1)} custom-call(f32[1,128,128]{2,1,0:T(8,128)S(1)} %fusion.18), custom_call_target="InvertDiagBlocksLowerTriangular" | custom-call | tf_op jit(solution)/shard_map/jit(_solve_triangular)/triangular_solve | solution.py:44
  564.3 2.3 convolution_select_fusion.2
  566.5 1.5 broadcast_select_fusion.1
  568.1 110.4 %all-reduce.9.cloned.1.call-done = f32[1024,128]{0,1:T(8,128)} async-done(((f32[1024,128]{0,1:T(8,128)}), f32[1024,128]{0,1:T(8,128)}) %all-reduce.9.cloned.1.call-update) | async-done | bytes 524304 | tf_op jit(solution)/shard_map/psum | solution.py:11
  678.8 9.3 %all-gather.12.cloned.1.call-done = f32[2048,128]{0,1:T(8,128)} async-done(((f32[1024,128]{0,1:T(8,128)}), f32[2048,128]{0,1:T(8,128)}) %all-gather.12.cloned.1.call-update) | async-done | bytes 1048592 | tf_op jit(solution)/shard_map/all_gather | solution.py:41
  689.9 11.7 %cholesky.96 = f32[128,128]{1,0:T(8,128)S(1)} custom-call(f32[128,128]{1,0:T(8,128)S(1)} %fusion.24), custom_call_target="Cholesky" | custom-call | tf_op jit(solution)/shard_map/jit(cholesky)/cholesky | solution.py:43
  703.0 9.8 %custom-call.10 = f32[1,128,128]{1,2,0:T(8,128)S(1)} custom-call(f32[1,128,128]{2,1,0:T(8,128)S(1)} %fusion.19), custom_call_target="InvertDiagBlocksLowerTriangular" | custom-call | tf_op jit(solution)/shard_map/jit(_solve_triangular)/triangular_solve | solution.py:44
  712.8 2.3 convolution_select_fusion.1
  715.0 1.5 broadcast_select_fusion
  716.8 110.1 %all-reduce.11.cloned.1.call-done = f32[1024,128]{0,1:T(8,128)} async-done(((f32[1024,128]{0,1:T(8,128)}), f32[1024,128]{0,1:T(8,128)}) %all-reduce.11.cloned.1.call-update) | async-done | bytes 524304 | tf_op jit(solution)/shard_map/psum | solution.py:11
  827.0 9.6 %all-gather.14.cloned.1.call-done = f32[2048,128]{0,1:T(8,128)} async-done(((f32[1024,128]{0,1:T(8,128)}), f32[2048,128]{0,1:T(8,128)}) %all-gather.14.cloned.1.call-update) | async-done | bytes 1048592 | tf_op jit(solution)/shard_map/all_gather | solution.py:41
  838.4 11.7 %cholesky.107 = f32[128,128]{1,0:T(8,128)S(1)} custom-call(f32[128,128]{1,0:T(8,128)S(1)} %fusion.22), custom_call_target="Cholesky" | custom-call | tf_op jit(solution)/shard_map/jit(cholesky)/cholesky | solution.py:43
  851.4 9.8 %custom-call.11 = f32[1,128,128]{1,2,0:T(8,128)S(1)} custom-call(f32[1,128,128]{2,1,0:T(8,128)S(1)} %fusion.20), custom_call_target="InvertDiagBlocksLowerTriangular" | custom-call | tf_op jit(solution)/shard_map/jit(_solve_triangular)/triangular_solve | solution.py:44
  861.3 2.3 convolution_select_fusion
  864.2 1.0 copy.22
  (50 shorter events, 16.1 us)
Async XLA Ops:
  6.5 14.1 %all-gather.6.cloned.1.call-start = ((), (), s32[]{:S(2)}) async-start(), calls=%async_computation.1 | async-start | bytes 1572864 | tf_op jit(solution)/shard_map/all_gather | solution.py:23
  27.4 166.1 %all-to-all-start = ((f32[1024,16,128]{2,0,1:T(8,128)}), f32[1024,16,128]{2,0,1:T(8,128)}, u32[]{:S(2)}, u32[]{:S(2)}) async-start(f32[1024,16,128]{2,0,1:T(8,128)} %bitcast.71), calls=%async_computation | async-start | bytes 16777216 | tf_op jit(solution)/shard_map/all_to_all | solution.py:27
  34.2 347.4 %all-reduce.5.cloned.1.call-start = ((), (), s32[]{:S(2)}) async-start(), calls=%async_computation.2 | async-start | bytes 1048576 | tf_op jit(solution)/shard_map/psum | solution.py:11
  270.9 120.4 %all-gather.8.cloned.1.call-start = ((), (), s32[]{:S(2)}) async-start(), calls=%async_computation.3 | async-start | bytes 1572864 | tf_op jit(solution)/shard_map/all_gather | solution.py:41
  381.7 148.5 %all-reduce.7.cloned.1.call-start = ((), (), s32[]{:S(2)}) async-start(), calls=%async_computation.4 | async-start | bytes 1048576 | tf_op jit(solution)/shard_map/psum | solution.py:11
  419.8 119.9 %all-gather.10.cloned.1.call-start = ((), (), s32[]{:S(2)}) async-start(), calls=%async_computation.5 | async-start | bytes 1572864 | tf_op jit(solution)/shard_map/all_gather | solution.py:41
  530.2 148.3 %all-reduce.9.cloned.1.call-start = ((), (), s32[]{:S(2)}) async-start(), calls=%async_computation.6 | async-start | bytes 1048576 | tf_op jit(solution)/shard_map/psum | solution.py:11
  568.0 120.1 %all-gather.12.cloned.1.call-start = ((), (), s32[]{:S(2)}) async-start(), calls=%async_computation.7 | async-start | bytes 1572864 | tf_op jit(solution)/shard_map/all_gather | solution.py:41
  678.5 148.5 %all-reduce.11.cloned.1.call-start = ((), (), s32[]{:S(2)}) async-start(), calls=%async_computation.8 | async-start | bytes 1048576 | tf_op jit(solution)/shard_map/psum | solution.py:11
  716.5 120.1 %all-gather.14.cloned.1.call-start = ((), (), s32[]{:S(2)}) async-start(), calls=%async_computation.9 | async-start | bytes 1572864 | tf_op jit(solution)/shard_map/all_gather | solution.py:41
Sparse Core Ops, SparseCore 0:
  8.9 11.7 all-gather.5
  271.0 110.6 all-reduce.4
  383.2 8.0 all-gather.7
  419.9 110.2 all-reduce.6
  531.6 8.0 all-gather.9
  568.2 110.2 all-reduce.8
  680.0 8.0 all-gather.11
  716.6 110.2 all-reduce.10
  828.5 8.0 all-gather.13
where the time goes:
time: 873 us; the launch traced here: 872 us
  waiting for transfers between devices  653 us (75%)
  other arithmetic  100 us (11%)
  blocking collectives  70.9 us (8%)
  matrix products  16.8 us (2%)
  between operations  14.1 us (2%)
  local copies, waits for them, and re-layouts  8.97 us (1%)
    psum x4, waiting for transfers between devices, spread(): return lax.psum(block, axis)  442 us
    all_to_all x1, waiting for transfers between devices, shards(): lax.all_to_all(partial_rows, 'tok', split_axis=1, concat_axis=0, tiled=True)  159 us
    psum x1, blocking collectives, shards(): lax.psum(jnp.sum(jnp.where(on_diag, hessian_tile, 0.0)), ('tok', 'blk'))  70.9 us
    another operation x12, other arithmetic, shards(): factor = jnp.linalg.cholesky(pivot_block)  49.6 us
    another operation x8, other arithmetic, shards(): solved = jax.scipy.linalg.solve_triangular(factor, column.T, lower=True).T  41.9 us
    all_gather x4, waiting for transfers between devices, shards(): column = lax.all_gather(strip_rows, 'blk', axis=0, tiled=True)  37.6 us
  transfers between devices with their start and end apart: 10, of which 10 were waited for; matrix products, arithmetic and copies ran while one was open for 0% of the time, Pallas kernels for 0%

commit v1 on v0

--- a/solution.py
+++ b/solution.py
@@ -8,7 +8,7 @@
 
 def spread(block, axis, holder):
     block = jnp.where(lax.axis_index(axis) == holder, block, jnp.zeros_like(block))
-    return lax.psum(block, axis)
+    return jnp.sum(lax.all_gather(block, axis), axis=0)
 
 
 def shards(activations):

time: 873 us -> 925 us (1.060)
  local copies, waits for them, and re-layouts: 8.97 us -> 40.6 us
  other arithmetic: 100 us -> 112 us
    all_gather x0 -> x4, waiting for transfers between devices: none -> 454 us  [spread(): return jnp.sum(lax.all_gather(block, axis), axis=0)]
    psum x4 -> x0, waiting for transfers between devices: 442 us -> none  [spread(): return lax.psum(block, axis)]
    unnamed x0 -> x3, local copies, waits for them, and re-layouts: none -> 29.6 us
    reduce_sum x0 -> x4, other arithmetic: none -> 11.9 us  [spread(): return jnp.sum(lax.all_gather(block, axis), axis=0)]
where the time goes in v1:
time: 925 us; the launch traced here: 920 us
  waiting for transfers between devices  657 us (71%)
  other arithmetic  112 us (12%)
  blocking collectives  70.9 us (8%)
  local copies, waits for them, and re-layouts  40.6 us (4%)
  matrix products  16.8 us (2%)
  between operations  14.6 us (2%)
    all_gather x4, waiting for transfers between devices, spread(): return jnp.sum(lax.all_gather(block, axis), axis=0)  454 us
    all_to_all x1, waiting for transfers between devices, shards(): lax.all_to_all(partial_rows, 'tok', split_axis=1, concat_axis=0, tiled=True)  159 us
    psum x1, blocking collectives, shards(): lax.psum(jnp.sum(jnp.where(on_diag, hessian_tile, 0.0)), ('tok', 'blk'))  70.9 us
    another operation x12, other arithmetic, shards(): factor = jnp.linalg.cholesky(pivot_block)  49.8 us
    another operation x8, other arithmetic, shards(): solved = jax.scipy.linalg.solve_triangular(factor, column.T, lower=True).T  41.9 us
    all_gather x4, waiting for transfers between devices, shards(): column = lax.all_gather(strip_rows, 'blk', axis=0, tiled=True)  29.7 us
    unnamed x3, local copies, waits for them, and re-layouts  29.6 us
  transfers between devices with their start and end apart: 10, of which 10 were waited for; matrix products, arithmetic and copies ran while one was open for 0% of the time, Pallas kernels for 0%

profile of v1, /device:TPU:0, one launch (start us, length us, event | category | flops | bytes accessed | tf_op | source)
XLA Modules:
  0.0 920.3 jit_solution(16311745096319215722)
XLA Ops:
  7.3 13.4 %all-gather.13.cloned.1.call-done = bf16[256,2048]{1,0:T(8,128)(2,1)} async-done(((bf16[256,1024]{1,0:T(8,128)(2,1)}), bf16[256,2048]{1,0:T(8,128)(2,1)}) %all-gather.13.cloned.1.call-update) | async-done | bytes 1048592 | tf_op jit(solution)/shard_map/all_gather | solution.py:23
  20.7 2.7 convolution_bitcast_fusion
  23.3 4.1 copy.48
  27.4 6.8 all-to-all-start
  34.3 159.2 %all-to-all-done = f32[1024,16,128]{2,0,1:T(8,128)} async-done(((f32[1024,16,128]{2,0,1:T(8,128)}), f32[1024,16,128]{2,0,1:T(8,128)}, u32[]{:S(2)}, u32[]{:S(2)}) %all-to-all-start) | async-done | bytes 8388640 | tf_op jit(solution)/shard_map/all_to_all | solution.py:27
  193.5 3.8 reduce_sum.54
  198.4 70.9 %psum.7 = f32[]{:T(128)} all-reduce(f32[]{:T(128)} %fusion.10), channel_id=1, replica_groups=mesh['tok'=16,'blk'=2] {'tok','blk'}, use_global_device_ids=true, to_apply=%region_2.3 | all-reduce | flops 1 | bytes 8 | tf_op jit(solution)/shard_map/psum | solution.py:36
  271.1 114.0 %all-gather.15.cloned.1.call-done = f32[16,1024,128]{2,1,0:T(8,128)} async-done(((f32[1,1024,128]{2,1,0:T(8,128)}), f32[16,1024,128]{2,1,0:T(8,128)}) %all-gather.15.cloned.1.call-update) | async-done | bytes 8388624 | tf_op jit(solution)/shard_map/all_gather | solution.py:11
  385.1 3.8 reduce_sum.56
  390.2 7.1 all-gather.17.cloned.1.call-done
  399.1 11.7 %cholesky.74 = f32[128,128]{1,0:T(8,128)S(1)} custom-call(f32[128,128]{1,0:T(8,128)S(1)} %fusion.28), custom_call_target="Cholesky" | custom-call | tf_op jit(solution)/shard_map/jit(cholesky)/cholesky | solution.py:43
  412.1 9.8 %custom-call.8 = f32[1,128,128]{1,2,0:T(8,128)S(1)} custom-call(f32[1,128,128]{2,1,0:T(8,128)S(1)} %fusion.17), custom_call_target="InvertDiagBlocksLowerTriangular" | custom-call | tf_op jit(solution)/shard_map/jit(_solve_triangular)/triangular_solve | solution.py:44
  426.0 113.2 %all-gather.25.cloned.1.call-done = f32[16384,128]{0,1:T(8,128)} async-done(((f32[1024,128]{0,1:T(8,128)}), f32[16384,128]{0,1:T(8,128)}) %all-gather.25.cloned.1.call-update) | async-done | bytes 8388624 | tf_op jit(solution)/shard_map/all_gather | solution.py:11
  539.3 9.9 %copy.44 = f32[16,8,16,1024]{3,2,1,0:T(8,128)S(1)} copy(f32[16,8,16,1024]{3,1,2,0:T(8,128)} %bitcast.91) | data formatting | bytes 16777216
  549.1 2.7 bitcast_reduce_fusion.2
  552.4 7.3 all-gather.19.cloned.1.call-done
  561.5 11.7 %cholesky.85 = f32[128,128]{1,0:T(8,128)S(1)} custom-call(f32[128,128]{1,0:T(8,128)S(1)} %fusion.26), custom_call_target="Cholesky" | custom-call | tf_op jit(solution)/shard_map/jit(cholesky)/cholesky | solution.py:43
  574.5 9.8 %custom-call.9 = f32[1,128,128]{1,2,0:T(8,128)S(1)} custom-call(f32[1,128,128]{2,1,0:T(8,128)S(1)} %fusion.18), custom_call_target="InvertDiagBlocksLowerTriangular" | custom-call | tf_op jit(solution)/shard_map/jit(_solve_triangular)/triangular_solve | solution.py:44
  588.3 113.3 %all-gather.27.cloned.1.call-done = f32[16384,128]{0,1:T(8,128)} async-done(((f32[1024,128]{0,1:T(8,128)}), f32[16384,128]{0,1:T(8,128)}) %all-gather.27.cloned.1.call-update) | async-done | bytes 8388624 | tf_op jit(solution)/shard_map/all_gather | solution.py:11
  701.6 9.9 %copy.45 = f32[16,8,16,1024]{3,2,1,0:T(8,128)S(1)} copy(f32[16,8,16,1024]{3,1,2,0:T(8,128)} %bitcast.92) | data formatting | bytes 16777216
  711.5 2.7 bitcast_reduce_fusion.1
  714.5 7.5 all-gather.21.cloned.1.call-done
  723.9 11.7 %cholesky.96 = f32[128,128]{1,0:T(8,128)S(1)} custom-call(f32[128,128]{1,0:T(8,128)S(1)} %fusion.24), custom_call_target="Cholesky" | custom-call | tf_op jit(solution)/shard_map/jit(cholesky)/cholesky | solution.py:43
  736.9 9.8 %custom-call.10 = f32[1,128,128]{1,2,0:T(8,128)S(1)} custom-call(f32[1,128,128]{2,1,0:T(8,128)S(1)} %fusion.19), custom_call_target="InvertDiagBlocksLowerTriangular" | custom-call | tf_op jit(solution)/shard_map/jit(_solve_triangular)/triangular_solve | solution.py:44
  746.7 2.3 convolution_select_fusion.1
  750.8 113.2 %all-gather.29.cloned.1.call-done = f32[16384,128]{0,1:T(8,128)} async-done(((f32[1024,128]{0,1:T(8,128)}), f32[16384,128]{0,1:T(8,128)}) %all-gather.29.cloned.1.call-update) | async-done | bytes 8388624 | tf_op jit(solution)/shard_map/all_gather | solution.py:11
  864.0 9.9 %copy.46 = f32[16,8,16,1024]{3,2,1,0:T(8,128)S(1)} copy(f32[16,8,16,1024]{3,1,2,0:T(8,128)} %bitcast.93) | data formatting | bytes 16777216
  873.9 2.7 bitcast_reduce_fusion
  876.6 7.8 all-gather.23.cloned.1.call-done
  886.2 12.0 %cholesky.107 = f32[128,128]{1,0:T(8,128)S(1)} custom-call(f32[128,128]{1,0:T(8,128)S(1)} %fusion.22), custom_call_target="Cholesky" | custom-call | tf_op jit(solution)/shard_map/jit(cholesky)/cholesky | solution.py:43
  899.5 9.8 %custom-call.11 = f32[1,128,128]{1,2,0:T(8,128)S(1)} custom-call(f32[1,128,128]{2,1,0:T(8,128)S(1)} %fusion.20), custom_call_target="InvertDiagBlocksLowerTriangular" | custom-call | tf_op jit(solution)/shard_map/jit(_solve_triangular)/triangular_solve | solution.py:44
  909.4 2.3 convolution_select_fusion
  (59 shorter events, 29.1 us)
Async XLA Ops:
  6.5 14.1 %all-gather.13.cloned.1.call-start = ((), (), s32[]{:S(2)}) async-start(), calls=%async_computation.1 | async-start | bytes 1572864 | tf_op jit(solution)/shard_map/all_gather | solution.py:23
  27.4 166.1 %all-to-all-start = ((f32[1024,16,128]{2,0,1:T(8,128)}), f32[1024,16,128]{2,0,1:T(8,128)}, u32[]{:S(2)}, u32[]{:S(2)}) async-start(f32[1024,16,128]{2,0,1:T(8,128)} %bitcast.90), calls=%async_computation | async-start | bytes 16777216 | tf_op jit(solution)/shard_map/all_to_all | solution.py:27
  34.2 350.8 %all-gather.15.cloned.1.call-start = ((), (), s32[]{:S(2)}) async-start(), calls=%async_computation.2 | async-start | bytes 8912896 | tf_op jit(solution)/shard_map/all_gather | solution.py:11
  271.1 126.2 %all-gather.17.cloned.1.call-start = ((), (), s32[]{:S(2)}) async-start(), calls=%async_computation.3 | async-start | bytes 1572864 | tf_op jit(solution)/shard_map/all_gather | solution.py:41
  389.9 149.3 %all-gather.25.cloned.1.call-start = ((), (), s32[]{:S(2)}) async-start(), calls=%async_computation.7 | async-start | bytes 8912896 | tf_op jit(solution)/shard_map/all_gather | solution.py:11
  425.7 133.9 %all-gather.19.cloned.1.call-start = ((), (), s32[]{:S(2)}) async-start(), calls=%async_computation.4 | async-start | bytes 1572864 | tf_op jit(solution)/shard_map/all_gather | solution.py:41
  551.9 149.8 %all-gather.27.cloned.1.call-start = ((), (), s32[]{:S(2)}) async-start(), calls=%async_computation.8 | async-start | bytes 8912896 | tf_op jit(solution)/shard_map/all_gather | solution.py:11
  588.1 134.0 %all-gather.21.cloned.1.call-start = ((), (), s32[]{:S(2)}) async-start(), calls=%async_computation.5 | async-start | bytes 1572864 | tf_op jit(solution)/shard_map/all_gather | solution.py:41
  714.2 149.8 %all-gather.29.cloned.1.call-start = ((), (), s32[]{:S(2)}) async-start(), calls=%async_computation.9 | async-start | bytes 8912896 | tf_op jit(solution)/shard_map/all_gather | solution.py:11
  750.5 134.0 %all-gather.23.cloned.1.call-start = ((), (), s32[]{:S(2)}) async-start(), calls=%async_computation.6 | async-start | bytes 1572864 | tf_op jit(solution)/shard_map/all_gather | solution.py:41
Sparse Core Ops, SparseCore 0:
  8.9 11.7 all-gather.12
  271.2 113.8 all-gather.14
  390.0 7.1 all-gather.16
  425.9 113.3 all-gather.24
  552.0 7.6 all-gather.18
  588.2 113.3 all-gather.26
  714.4 7.6 all-gather.20
  750.6 113.3 all-gather.28
  876.7 7.6 all-gather.22
